TPU v7x, 32 devices: a whole 2x2x4 slice. The times are simulated.
32 devices in a mesh: grp: 4 (over x, core), gx: 2 (over y), gy: 4 (over z).
Axes of the slice: x: 2, y: 2, z: 4, core: 2. Of those that a mesh axis runs over, the one named last changes fastest.
Arguments:
- pressure: float32 [24, 128, 1024], P(None, ('grp', 'gy'), 'gx'), may hold values from -2 to 0.2
- soil_class: int32 [24, 128, 1024], P(None, ('grp', 'gy'), 'gx'), may hold values from 0 to 11
- capacity_range: float32 [12], replicated, may hold values from 0.25 to 0.45
- inverse_entry: float32 [12], replicated, may hold values from 0.3 to 3
- shape_index: float32 [12], replicated, may hold values from 1.3 to 2.5
- conductivity: float32 [12], replicated, may hold values from 0.05 to 1
- depth: float32 [128, 1024], P('grp', ('gx', 'gy')), may hold values from 0 to 2
- elevation: float32 [128, 1024], P('grp', ('gx', 'gy')), may hold values from -4 to 4
- roughness: float32 [128, 1024], P('grp', ('gx', 'gy')), may hold values from 2 to 8
- rain: float32 [128, 1024], P('grp', ('gx', 'gy')), may hold values from 0.1 to 1
- land_mask: int32 [128, 1024], P('grp', ('gx', 'gy')), may hold values 0 or 1
- channel_mask: int32 [128, 1024], P('grp', ('gx', 'gy')), may hold values 0 or 1
Outputs:
- head: float32 [24, 128, 1024], P(None, ('grp', 'gy'), 'gx')
- water: float32 [128, 1024], P('grp', ('gx', 'gy'))
All inputs are finite; a program needn't handle non-finite values. No bound on the sum of `land_mask` or of `channel_mask` on one device may be relied on, other than what follows from the above.
Results may differ from a plain program's by a relative error of at most 0.0003.
Values sent between devices are 32-bit elements; how exact they have to be, the bound alone decides.
No kernel may reach another device: no remote copies, remote signals or barrier semaphores. Data moves between devices by JAX's collectives and lax.ppermute only.
A program may use at most 64 MiB of HBM per device.

v0:
```python
import jax
import jax.numpy as jnp
from jax import lax
from jax.sharding import PartitionSpec as P

SWEEPS = 2
PASSES = 3
STORAGE = 0.01
LATERAL = 4.0
VERTICAL = 4.0
GRAVITY_STEP = 0.5
SUCTION_FLOOR = 0.01
SLOPE_FLOOR = 0.1
SURFACE_STEP = 0.3
LEAKANCE = 0.5
SOURCE_GAIN = 1.0


def with_halo(shard, sides, width):
    for axis, dim in sides:
        size, length = (lax.axis_size(axis), shard.shape[dim])
        up = [(i, (i + 1) % size) for i in range(size - 1)]
        down = [(j, i) for i, j in up]
        last = lax.slice_in_dim(shard, length - width, length, axis=dim)
        leading = lax.slice_in_dim(shard, 0, width, axis=dim)
        before = lax.ppermute(last, axis, up)
        after = lax.ppermute(leading, axis, down)
        shard = jnp.concatenate([before, shard, after], axis=dim)
    return shard


def lookup(soil_class, tables):
    results = []
    for table in tables:
        filled = jnp.zeros(soil_class.shape, table.dtype)
        for kind_number in range(table.shape[0]):
            filled = jnp.where(soil_class == kind_number, table[kind_number], filled)
        results.append(filled)
    return results


def closures(pressure, capacity_range, inverse_entry, pore_index, conductivity):
    exponent = 1.0 / (1.0 - pore_index)
    scaled = jnp.maximum(-inverse_entry * pressure, SUCTION_FLOOR)
    log_scaled = jnp.log(scaled)
    log_sum = jnp.log1p(jnp.exp(exponent * log_scaled))
    saturation = jnp.exp(-pore_index * log_sum)
    content = capacity_range * saturation
    capacity = STORAGE + capacity_range * pore_index * exponent * inverse_entry * jnp.exp(
        (exponent - 1.0) * log_scaled - (pore_index + 1.0) * log_sum
    )
    conduct = (
        conductivity
        * jnp.sqrt(saturation)
        * jnp.square(1.0 - jnp.exp(pore_index * (exponent * log_scaled - log_sum)))
    )
    return (content, capacity, conduct)


def update_cells(padded, conduct_pad, capacity, content_gap, source):
    layers = padded.shape[0] - 2
    rows = padded.shape[1] - 2
    cols = padded.shape[2] - 2
    center = padded[1:-1, 1:-1, 1:-1]
    own_conduct = conduct_pad[1:-1, 1:-1, 1:-1]
    numerator = capacity * center - content_gap
    denominator = capacity
    neighbours = (
        (1, 0, 1, LATERAL, 0.0),
        (1, 2, 1, LATERAL, 0.0),
        (1, 1, 0, LATERAL, 0.0),
        (1, 1, 2, LATERAL, 0.0),
        (0, 1, 1, VERTICAL, GRAVITY_STEP),
        (2, 1, 1, VERTICAL, -GRAVITY_STEP),
    )
    for first, second, third, weight, offset in neighbours:
        beside = padded[first : first + layers, second : second + rows, third : third + cols]
        beside_conduct = conduct_pad[
            first : first + layers, second : second + rows, third : third + cols
        ]
        face_weight = weight * jnp.sqrt(own_conduct * beside_conduct)
        numerator = numerator + face_weight * (beside + offset)
        denominator = denominator + face_weight
    gained = jnp.concatenate(
        [(SOURCE_GAIN * source)[None], jnp.zeros((layers - 1, rows, cols), source.dtype)], axis=0
    )
    numerator = numerator + gained
    return numerator / denominator


def face_flux(upper_level, lower_level, upper_depth, lower_depth, upper_convey, lower_convey):
    slope = upper_level - lower_level
    upwind = jnp.where(slope >= 0, upper_depth, lower_depth)
    carried = upwind * jnp.cbrt(upwind * upwind)
    return (
        jnp.sqrt(upper_convey * lower_convey)
        * carried
        * slope
        / jnp.sqrt(jnp.maximum(jnp.abs(slope), SLOPE_FLOOR))
    )


def overland(depth_pad, level_pad, convey_pad, leak, top, rain):
    current = depth_pad[1:-1, 1:-1]
    surface = level_pad + depth_pad
    across = face_flux(
        surface[:-1, 1:-1],
        surface[1:, 1:-1],
        depth_pad[:-1, 1:-1],
        depth_pad[1:, 1:-1],
        convey_pad[:-1, 1:-1],
        convey_pad[1:, 1:-1],
    )
    along = face_flux(
        surface[1:-1, :-1],
        surface[1:-1, 1:],
        depth_pad[1:-1, :-1],
        depth_pad[1:-1, 1:],
        convey_pad[1:-1, :-1],
        convey_pad[1:-1, 1:],
    )
    outflow = across[1:] - across[:-1] + (along[:, 1:] - along[:, :-1])
    rate = leak * (current - top)
    return (jnp.maximum(current + SURFACE_STEP * (rain - rate - outflow), 0.0), rate)


def trim_edges(field, margin):
    rows = field.shape[-2]
    cols = field.shape[-1]
    return field[..., margin : rows - margin, margin : cols - margin]


def pad_layers(field):
    return jnp.pad(field, ((1, 1), (0, 0), (0, 0)))


def local(
    pressure,
    soil_class,
    capacity_range,
    inverse_entry,
    shape_index,
    conductivity,
    depth,
    elevation,
    roughness,
    rain,
    land_mask,
    channel_mask,
):
    pore_table = 1.0 - 1.0 / shape_index
    tables = (capacity_range, inverse_entry, pore_table, conductivity)
    range_cells, entry_cells, pore_cells, conduct_cells = lookup(soil_class, tables)
    content0, capacity, conduct = closures(
        pressure, range_cells, entry_cells, pore_cells, conduct_cells
    )
    top_conduct = conduct[0]
    top, top_surface = (
        lax.all_to_all(pressure[0], "gy", split_axis=1, concat_axis=0, tiled=True),
        lax.all_to_all(top_conduct, "gy", split_axis=1, concat_axis=0, tiled=True),
    )
    leak = LEAKANCE * land_mask.astype(jnp.float32) * top_surface
    convey = (1.0 + channel_mask.astype(jnp.float32)) / roughness
    exchange = jnp.zeros_like(depth)
    surface_pad = with_halo(
        jnp.stack([depth, elevation, convey, leak, top, rain]),
        (("grp", 1), (("gx", "gy"), 2)),
        PASSES,
    )
    water = surface_pad[0]
    for pass_number in range(PASSES):
        water, rate = overland(
            water,
            trim_edges(surface_pad[1], pass_number),
            trim_edges(surface_pad[2], pass_number),
            trim_edges(surface_pad[3], pass_number + 1),
            trim_edges(surface_pad[4], pass_number + 1),
            trim_edges(surface_pad[5], pass_number + 1),
        )
        exchange = exchange + SURFACE_STEP * trim_edges(rate, PASSES - pass_number - 1)
    source = lax.all_to_all(exchange, "gy", split_axis=0, concat_axis=1, tiled=True)
    head = pressure
    content = content0
    for sweep_number in range(SWEEPS):
        soil_rim = with_halo(jnp.stack([head, conduct]), ((("grp", "gy"), 2), ("gx", 3)), 1)
        head = update_cells(
            pad_layers(soil_rim[0]), pad_layers(soil_rim[1]), capacity, content - content0, source
        )
        if sweep_number + 1 < SWEEPS:
            content, capacity, conduct = closures(
                head, range_cells, entry_cells, pore_cells, conduct_cells
            )
    return (head, water)


def solution(mesh):
    return jax.shard_map(
        local,
        mesh=mesh,
        in_specs=(
            P(None, ("grp", "gy"), "gx"),
            P(None, ("grp", "gy"), "gx"),
            P(),
            P(),
            P(),
            P(),
            P("grp", ("gx", "gy")),
            P("grp", ("gx", "gy")),
            P("grp", ("gx", "gy")),
            P("grp", ("gx", "gy")),
            P("grp", ("gx", "gy")),
            P("grp", ("gx", "gy")),
        ),
        out_specs=(P(None, ("grp", "gy"), "gx"), P("grp", ("gx", "gy"))),
        check_vma=False,
    )
```

profile of v0, /device:TPU:1, one launch (start us, length us, event | category | flops | bytes accessed | tf_op | source)
XLA Modules:
  0.0 136.5 jit_solution(11352913227923329193)
XLA Ops:
  0.7 1.8 %fusion.114 = (f32[1]{0:T(128)}, f32[1]{0:T(128)}, f32[1]{0:T(128)}, f32[1]{0:T(128)}, f32[1]{0:T(128)}, /*index=5*/f32[1]{0:T(128)}, f32[1]{0:T(128)}, f32[1]{0...) fusion(f32[12]{0:T(128)} %param.15), kind=kLoop, calls=%fused_computation.231 | loop fusion | bytes 96 | tf_op jit(solution)/shard_map/slice | solution.py:37
  2.5 1.8 %fusion.113 = (f32[1]{0:T(128)}, f32[1]{0:T(128)}, f32[1]{0:T(128)}, f32[1]{0:T(128)}, f32[1]{0:T(128)}, /*index=5*/f32[1]{0:T(128)}, f32[1]{0:T(128)}, f32[1]{0...) fusion(f32[12]{0:T(128)} %param.17), kind=kLoop, calls=%fused_computation.230 | loop fusion | bytes 96 | tf_op jit(solution)/shard_map/slice | solution.py:37
  4.9 0.7 fusion.112
  5.6 26.2 %multiply_multiply_fusion = (f32[24,8,512]{2,1,0:T(8,128)S(1)}, f32[24,8,512]{2,1,0:T(8,128)S(1)}, f32[24,8,512]{2,1,0:T(8,128)S(1)}, f32[24,8,512]{2,1,0:T(8,12...) fusion(f32[24,8,512]{2,1,0:T(8,128)} %param.12, ...), kind=kLoop, calls=%fused_computation.100 | loop fusion | flops 6094848 | bytes 3539088 | tf_op jit(solution)/shard_map/mul | solution.py:53
  32.5 5.4 %all-to-all-start = ((f32[8,4,128]{2,0,1:T(8,128)}), f32[8,4,128]{2,0,1:T(8,128)S(1)}, u32[]{:S(2)}, u32[]{:S(2)}) async-start(f32[8,4,128]{2,0,1:T(8,128)} %slice_bitcast_fusion.10), calls=%async_computation | async-start | bytes 32768 | tf_op jit(solution)/shard_map/all_to_all | solution.py:160
  38.6 3.8 %all-to-all-done = f32[8,4,128]{2,0,1:T(8,128)S(1)} async-done(((f32[8,4,128]{2,0,1:T(8,128)}), f32[8,4,128]{2,0,1:T(8,128)S(1)}, u32[]{:S(2)}, u32[]{:S(2)}) %all-to-all-start) | async-done | bytes 16416 | tf_op jit(solution)/shard_map/all_to_all | solution.py:160
  42.3 3.2 %all-to-all-start.1 = ((f32[8,4,128]{2,0,1:T(8,128)}), f32[8,4,128]{2,0,1:T(8,128)S(1)}, u32[]{:S(2)}, u32[]{:S(2)}) async-start(f32[8,4,128]{2,0,1:T(8,128)} %slice_bitcast_fusion.11), calls=%async_computation.1 | async-start | bytes 32768 | tf_op jit(solution)/shard_map/all_to_all | solution.py:159
  45.6 4.4 %all-to-all-done.1 = f32[8,4,128]{2,0,1:T(8,128)S(1)} async-done(((f32[8,4,128]{2,0,1:T(8,128)}), f32[8,4,128]{2,0,1:T(8,128)S(1)}, u32[]{:S(2)}, u32[]{:S(2)}) %all-to-all-start.1) | async-done | bytes 16416 | tf_op jit(solution)/shard_map/all_to_all | solution.py:159
  50.1 5.2 %collective-permute-start.5 = (f32[6,3,128]{2,1,0:T(4,128)S(1)}, f32[6,3,128]{2,1,0:T(4,128)S(1)}, u32[]{:S(2)}, u32[]{:S(2)}) collective-permute-start(f32[6,3,128]{2,1,0:T(4,128)S(1)} %get-tuple-element.50), channel_id=1, source_target_pairs={{8,0},{16,8},{24,16},{9,1},{17,9},{25,17},{10,2},{18,10},{26,18},{... | collective-permute-start | bytes 27656 | tf_op jit(solution)/shard_map/ppermute | solution.py:27
  55.2 3.0 %collective-permute-start.4 = (f32[6,3,128]{2,1,0:T(4,128)S(1)}, f32[6,3,128]{2,1,0:T(4,128)S(1)}, u32[]{:S(2)}, u32[]{:S(2)}) collective-permute-start(f32[6,3,128]{2,1,0:T(4,128)S(1)} %get-tuple-element.49), channel_id=1, source_target_pairs={{0,8},{8,16},{16,24},{1,9},{9,17},{17,25},{2,10},{10,18},{18,26},{... | collective-permute-start | bytes 27656 | tf_op jit(solution)/shard_map/ppermute | solution.py:26
  58.4 1.9 %collective-permute-start.1 = (f32[2,24,1,512]{3,2,1,0:T(1,128)S(1)}, f32[2,24,1,512]{3,2,1,0:T(1,128)S(1)}, u32[]{:S(2)}, u32[]{:S(2)}) collective-permute-start(f32[2,24,1,512]{3,2,1,0:T(1,128)S(1)} %get-tuple-element.38), channel_id=1, source_target_pairs={{1,0},{2,1},{3,2},{8,3},{9,8},{10,9},{11,10},{16,11},{17,16},{18,1... | collective-permute-start | bytes 294920 | tf_op jit(solution)/shard_map/ppermute | solution.py:27
  60.3 3.4 %collective-permute-start = (f32[2,24,1,512]{3,2,1,0:T(1,128)S(1)}, f32[2,24,1,512]{3,2,1,0:T(1,128)S(1)}, u32[]{:S(2)}, u32[]{:S(2)}) collective-permute-start(f32[2,24,1,512]{3,2,1,0:T(1,128)S(1)} %get-tuple-element.37), channel_id=1, source_target_pairs={{0,1},{1,2},{2,3},{3,8},{8,9},{9,10},{10,11},{11,16},{16,17},{17,1... | collective-permute-start | bytes 294920 | tf_op jit(solution)/shard_map/ppermute | solution.py:26
  63.8 1.3 collective-permute-start.7
  65.1 4.0 %collective-permute-start.6 = (f32[6,38,3]{2,1,0:T(8,128)S(1)}, f32[6,38,3]{2,1,0:T(8,128)S(1)}, u32[]{:S(2)}, u32[]{:S(2)}) collective-permute-start(f32[6,38,3]{2,1,0:T(8,128)S(1)} %get-tuple-element.47), channel_id=1, source_target_pairs={{0,1},{1,2},{2,3},{3,4},{4,5},{5,6},{6,7},{8,9},{9,10},{10,11},{11... | collective-permute-start | bytes 8216 | tf_op jit(solution)/shard_map/ppermute | solution.py:26
  69.8 2.2 %collective-permute-done.7 = f32[6,38,3]{2,1,0:T(8,128)S(1)} collective-permute-done((f32[6,38,3]{2,1,0:T(8,128)S(1)}, f32[6,38,3]{2,1,0:T(8,128)S(1)}, u32[]{:S(2)}, u32[]{:S(2)}) %collective-permute-start.7) | collective-permute-done | bytes 2768 | tf_op jit(solution)/shard_map/ppermute | solution.py:27
  74.1 1.3 collective-permute-start.3
  75.4 9.5 %collective-permute-start.2 = (f32[2,24,10,1]{3,2,1,0:T(8,128)S(1)}, f32[2,24,10,1]{3,2,1,0:T(8,128)S(1)}, u32[]{:S(2)}, u32[]{:S(2)}) collective-permute-start(f32[2,24,10,1]{3,2,1,0:T(8,128)S(1)} %get-tuple-element.33), channel_id=1, source_target_pairs={{0,4},{1,5},{2,6},{3,7},{8,12},{9,13},{10,14},{11,15},{16,20},{17,... | collective-permute-start | bytes 5768 | tf_op jit(solution)/shard_map/ppermute | solution.py:26
  84.8 0.7 fusion.96
  85.5 3.2 %all-to-all-start.2 = ((f32[4,8,128]{2,1,0:T(8,128)}), f32[4,8,128]{2,1,0:T(8,128)S(1)}, u32[]{:S(2)}, u32[]{:S(2)}) async-start(f32[4,8,128]{2,1,0:T(8,128)} %get-tuple-element.46), calls=%async_computation.2 | async-start | bytes 32768 | tf_op jit(solution)/shard_map/all_to_all | solution.py:181
  88.8 3.2 %collective-permute-done.3 = f32[2,24,10,1]{3,2,1,0:T(8,128)S(1)} collective-permute-done((f32[2,24,10,1]{3,2,1,0:T(8,128)S(1)}, f32[2,24,10,1]{3,2,1,0:T(8,128)S(1)}, u32[]{:S(2)}, u32[]{:S(2)}) %collective-permute-start.3) | collective-permute-done | bytes 1952 | tf_op jit(solution)/shard_map/ppermute | solution.py:27
  92.0 0.9 collective-permute-done.2
  92.9 2.4 %pad_maximum_fusion = f32[2,24,10,514]{3,2,1,0:T(8,128)S(1)} fusion(f32[2,24,10,1]{3,2,1,0:T(8,128)S(1)} %collective-permute-done.3, f32[2,24,1,512]{3,2,1,0:T(1,128)} %copy-done.1, f32[1,24,8,512]{3,2,1,0:T(8,128)S(1)} %bitcast.118, f32[1,24,8,512]{3,2,1,0:T(8,128)S(1)} %bitcast.112, f32[2,24,1,512]{3,2,1,0:T(1,128)} %copy-done.2, ...), kind=kLoop, calls=%fused_computation | loop fusion | flops 1233600 | bytes 1973760 | tf_op jit(solution)/shard_map/concatenate | solution.py:28
  95.4 11.8 %multiply_bitcast_fusion = (f32[1,24,8,512]{3,2,1,0:T(8,128)S(1)}, f32[24,8,512]{2,1,0:T(8,128)S(1)}, f32[24,8,512]{2,1,0:T(8,128)S(1)}) fusion(f32[24,8,512]{2,1,0:T(8,128)S(1)} %get-tuple-element.14, f32[24,8,512]{2,1,0:T(8,128)S(1)} %get-tuple-element.13, f32[24,8,512]{2,1,0:T(8,128)S(1)} %get-tuple-element.12, f32[1,8,512]{2,1,0:T(8,128)S(1)} %bitcast.119, ...), kind=kLoop, calls=%fused_computation.94 | loop fusion | flops 7667712 | bytes 9846832 | tf_op jit(solution)/shard_map/stack | solution.py:185
  107.4 3.4 %collective-permute-start.9 = (f32[2,24,1,512]{3,2,1,0:T(1,128)S(1)}, f32[2,24,1,512]{3,2,1,0:T(1,128)S(1)}, u32[]{:S(2)}, u32[]{:S(2)}) collective-permute-start(f32[2,24,1,512]{3,2,1,0:T(1,128)S(1)} %get-tuple-element.36), channel_id=1, source_target_pairs={{1,0},{2,1},{3,2},{8,3},{9,8},{10,9},{11,10},{16,11},{17,16},{18,1... | collective-permute-start | bytes 294920 | tf_op jit(solution)/shard_map/ppermute | solution.py:27
  110.8 1.9 %collective-permute-start.8 = (f32[2,24,1,512]{3,2,1,0:T(1,128)S(1)}, f32[2,24,1,512]{3,2,1,0:T(1,128)S(1)}, u32[]{:S(2)}, u32[]{:S(2)}) collective-permute-start(f32[2,24,1,512]{3,2,1,0:T(1,128)S(1)} %get-tuple-element.35), channel_id=1, source_target_pairs={{0,1},{1,2},{2,3},{3,8},{8,9},{9,10},{10,11},{11,16},{16,17},{17,1... | collective-permute-start | bytes 294920 | tf_op jit(solution)/shard_map/ppermute | solution.py:26
  112.7 6.4 %collective-permute-done.8 = f32[2,24,1,512]{3,2,1,0:T(1,128)S(1)} collective-permute-done((f32[2,24,1,512]{3,2,1,0:T(1,128)S(1)}, f32[2,24,1,512]{3,2,1,0:T(1,128)S(1)}, u32[]{:S(2)}, u32[]{:S(2)}) %collective-permute-start.8) | collective-permute-done | bytes 98336 | tf_op jit(solution)/shard_map/ppermute | solution.py:26
  119.4 1.3 collective-permute-start.11
  120.7 4.3 %collective-permute-start.10 = (f32[2,24,10,1]{3,2,1,0:T(8,128)S(1)}, f32[2,24,10,1]{3,2,1,0:T(8,128)S(1)}, u32[]{:S(2)}, u32[]{:S(2)}) collective-permute-start(f32[2,24,10,1]{3,2,1,0:T(8,128)S(1)} %get-tuple-element.31), channel_id=1, source_target_pairs={{0,4},{1,5},{2,6},{3,7},{8,12},{9,13},{10,14},{11,15},{16,20},{17,... | collective-permute-start | bytes 5768 | tf_op jit(solution)/shard_map/ppermute | solution.py:26
  125.1 5.0 %collective-permute-done.11 = f32[2,24,10,1]{3,2,1,0:T(8,128)S(1)} collective-permute-done((f32[2,24,10,1]{3,2,1,0:T(8,128)S(1)}, f32[2,24,10,1]{3,2,1,0:T(8,128)S(1)}, u32[]{:S(2)}, u32[]{:S(2)}) %collective-permute-start.11) | collective-permute-done | bytes 1952 | tf_op jit(solution)/shard_map/ppermute | solution.py:27
  130.1 1.8 %collective-permute-done.10 = f32[2,24,10,1]{3,2,1,0:T(8,128)S(1)} collective-permute-done((f32[2,24,10,1]{3,2,1,0:T(8,128)S(1)}, f32[2,24,10,1]{3,2,1,0:T(8,128)S(1)}, u32[]{:S(2)}, u32[]{:S(2)}) %collective-permute-start.10) | collective-permute-done | bytes 1952 | tf_op jit(solution)/shard_map/ppermute | solution.py:26
  131.8 1.4 %pad_maximum_fusion.1 = f32[2,24,10,514]{3,2,1,0:T(8,128)S(1)} fusion(f32[2,24,10,1]{3,2,1,0:T(8,128)S(1)} %collective-permute-done.11, f32[2,24,1,512]{3,2,1,0:T(1,128)S(1)} %collective-permute-done.9, f32[1,24,8,512]{3,2,1,0:T(8,128)S(1)} %get-tuple-element.5, f32[1,24,8,512]{3,2,1,0:T(8,128)S(1)} %bitcast.115, ...), kind=kLoop, calls=%fused_computation.1 | loop fusion | flops 1233600 | bytes 1973760 | tf_op jit(solution)/shard_map/concatenate | solution.py:28
  133.4 3.1 %fusion.1 = f32[24,8,512]{2,1,0:T(8,128)} fusion(f32[1,8,512]{2,1,0:T(8,128)S(1)} %bitcast.120, f32[24,10,514]{2,1,0:T(8,128)S(1)} %get-tuple-element.28, f32[24,10,514]{2,1,0:T(8,128)S(1)} %get-tuple-element.27, f32[24,8,512]{2,1,0:T(8,128)S(1)} %get-tuple-element.7, f32[24,8,512]{2,1,0:T(8,128)S(1)} %get-tuple-element.14, ...), kind=kLoop, calls=%fused_computation.17 | loop fusion | flops 5996544 | bytes 8273920 | tf_op jit(solution)/shard_map/div | solution.py:88
  (57 shorter events, 5.5 us)
Async XLA Ops:
  0.6 37.3 %copy-start = (f32[24,8,512]{2,1,0:T(8,128)S(1)}, f32[24,8,512]{2,1,0:T(8,128)}, u32[]{:S(2)}) copy-start(f32[24,8,512]{2,1,0:T(8,128)} %param.12) | copy-start | bytes 1179652
  0.6 37.2 %copy-start.7 = (f32[32,128]{1,0:T(8,128)S(1)}, f32[32,128]{1,0:T(8,128)}, u32[]{:S(2)}) copy-start(f32[32,128]{1,0:T(8,128)} %param.18) | copy-start | bytes 49156
  0.7 37.2 %copy-start.8 = (f32[32,128]{1,0:T(8,128)S(1)}, f32[32,128]{1,0:T(8,128)}, u32[]{:S(2)}) copy-start(f32[32,128]{1,0:T(8,128)} %param.19) | copy-start | bytes 49156
  0.7 37.2 %copy-start.4 = (f32[32,128]{1,0:T(8,128)S(1)}, f32[32,128]{1,0:T(8,128)}, u32[]{:S(2)}) copy-start(f32[32,128]{1,0:T(8,128)} %param.20) | copy-start | bytes 49156
  0.7 37.2 %copy-start.5 = (s32[32,128]{1,0:T(8,128)S(1)}, s32[32,128]{1,0:T(8,128)}, u32[]{:S(2)}) copy-start(s32[32,128]{1,0:T(8,128)} %param.23) | copy-start | bytes 49156
  5.6 40.0 %copy-start.6 = (s32[32,128]{1,0:T(8,128)S(1)}, s32[32,128]{1,0:T(8,128)}, u32[]{:S(2)}) copy-start(s32[32,128]{1,0:T(8,128)} %param.22) | copy-start | bytes 49156
  5.6 44.4 %copy-start.9 = (f32[32,128]{1,0:T(8,128)S(1)}, f32[32,128]{1,0:T(8,128)}, u32[]{:S(2)}) copy-start(f32[32,128]{1,0:T(8,128)} %param.21) | copy-start | bytes 49156
  5.6 63.5 %copy-start.3 = (f32[12]{0:T(128)S(1)}, f32[12]{0:T(128)}, u32[]{:S(2)}) copy-start(f32[12]{0:T(128)} %param.14) | copy-start | bytes 148
  32.5 9.9 %all-to-all-start = ((f32[8,4,128]{2,0,1:T(8,128)}), f32[8,4,128]{2,0,1:T(8,128)S(1)}, u32[]{:S(2)}, u32[]{:S(2)}) async-start(f32[8,4,128]{2,0,1:T(8,128)} %slice_bitcast_fusion.10), calls=%async_computation | async-start | bytes 32768 | tf_op jit(solution)/shard_map/all_to_all | solution.py:160
  42.3 7.7 %all-to-all-start.1 = ((f32[8,4,128]{2,0,1:T(8,128)}), f32[8,4,128]{2,0,1:T(8,128)S(1)}, u32[]{:S(2)}, u32[]{:S(2)}) async-start(f32[8,4,128]{2,0,1:T(8,128)} %slice_bitcast_fusion.11), calls=%async_computation.1 | async-start | bytes 32768 | tf_op jit(solution)/shard_map/all_to_all | solution.py:159
  50.1 13.6 %collective-permute-start.5 = (f32[6,3,128]{2,1,0:T(4,128)S(1)}, f32[6,3,128]{2,1,0:T(4,128)S(1)}, u32[]{:S(2)}, u32[]{:S(2)}) collective-permute-start(f32[6,3,128]{2,1,0:T(4,128)S(1)} %get-tuple-element.50), channel_id=1, source_target_pairs={{8,0},{16,8},{24,16},{9,1},{17,9},{25,17},{10,2},{18,10},{26,18},{... | collective-permute-start | bytes 27656 | tf_op jit(solution)/shard_map/ppermute | solution.py:27
  55.2 8.5 %collective-permute-start.4 = (f32[6,3,128]{2,1,0:T(4,128)S(1)}, f32[6,3,128]{2,1,0:T(4,128)S(1)}, u32[]{:S(2)}, u32[]{:S(2)}) collective-permute-start(f32[6,3,128]{2,1,0:T(4,128)S(1)} %get-tuple-element.49), channel_id=1, source_target_pairs={{0,8},{8,16},{16,24},{1,9},{9,17},{17,25},{2,10},{10,18},{18,26},{... | collective-permute-start | bytes 27656 | tf_op jit(solution)/shard_map/ppermute | solution.py:26
  58.4 15.0 %collective-permute-start.1 = (f32[2,24,1,512]{3,2,1,0:T(1,128)S(1)}, f32[2,24,1,512]{3,2,1,0:T(1,128)S(1)}, u32[]{:S(2)}, u32[]{:S(2)}) collective-permute-start(f32[2,24,1,512]{3,2,1,0:T(1,128)S(1)} %get-tuple-element.38), channel_id=1, source_target_pairs={{1,0},{2,1},{3,2},{8,3},{9,8},{10,9},{11,10},{16,11},{17,16},{18,1... | collective-permute-start | bytes 294920 | tf_op jit(solution)/shard_map/ppermute | solution.py:27
  60.3 13.1 %collective-permute-start = (f32[2,24,1,512]{3,2,1,0:T(1,128)S(1)}, f32[2,24,1,512]{3,2,1,0:T(1,128)S(1)}, u32[]{:S(2)}, u32[]{:S(2)}) collective-permute-start(f32[2,24,1,512]{3,2,1,0:T(1,128)S(1)} %get-tuple-element.37), channel_id=1, source_target_pairs={{0,1},{1,2},{2,3},{3,8},{8,9},{9,10},{10,11},{11,16},{16,17},{17,1... | collective-permute-start | bytes 294920 | tf_op jit(solution)/shard_map/ppermute | solution.py:26
  63.8 8.2 %collective-permute-start.7 = (f32[6,38,3]{2,1,0:T(8,128)S(1)}, f32[6,38,3]{2,1,0:T(8,128)S(1)}, u32[]{:S(2)}, u32[]{:S(2)}) collective-permute-start(f32[6,38,3]{2,1,0:T(8,128)S(1)} %get-tuple-element.48), channel_id=1, source_target_pairs={{1,0},{2,1},{3,2},{4,3},{5,4},{6,5},{7,6},{9,8},{10,9},{11,10},{12... | collective-permute-start | bytes 8216 | tf_op jit(solution)/shard_map/ppermute | solution.py:27
  65.1 6.9 %collective-permute-start.6 = (f32[6,38,3]{2,1,0:T(8,128)S(1)}, f32[6,38,3]{2,1,0:T(8,128)S(1)}, u32[]{:S(2)}, u32[]{:S(2)}) collective-permute-start(f32[6,38,3]{2,1,0:T(8,128)S(1)} %get-tuple-element.47), channel_id=1, source_target_pairs={{0,1},{1,2},{2,3},{3,4},{4,5},{5,6},{6,7},{8,9},{9,10},{10,11},{11... | collective-permute-start | bytes 8216 | tf_op jit(solution)/shard_map/ppermute | solution.py:26
  73.4 0.6 copy-start.1
  73.4 0.7 copy-start.2
  74.1 17.9 %collective-permute-start.3 = (f32[2,24,10,1]{3,2,1,0:T(8,128)S(1)}, f32[2,24,10,1]{3,2,1,0:T(8,128)S(1)}, u32[]{:S(2)}, u32[]{:S(2)}) collective-permute-start(f32[2,24,10,1]{3,2,1,0:T(8,128)S(1)} %get-tuple-element.34), channel_id=1, source_target_pairs={{4,0},{5,1},{6,2},{7,3},{12,8},{13,9},{14,10},{15,11},{20,16},{21,... | collective-permute-start | bytes 5768 | tf_op jit(solution)/shard_map/ppermute | solution.py:27
  75.4 17.6 %collective-permute-start.2 = (f32[2,24,10,1]{3,2,1,0:T(8,128)S(1)}, f32[2,24,10,1]{3,2,1,0:T(8,128)S(1)}, u32[]{:S(2)}, u32[]{:S(2)}) collective-permute-start(f32[2,24,10,1]{3,2,1,0:T(8,128)S(1)} %get-tuple-element.33), channel_id=1, source_target_pairs={{0,4},{1,5},{2,6},{3,7},{8,12},{9,13},{10,14},{11,15},{16,20},{17,... | collective-permute-start | bytes 5768 | tf_op jit(solution)/shard_map/ppermute | solution.py:26
  85.5 9.9 %all-to-all-start.2 = ((f32[4,8,128]{2,1,0:T(8,128)}), f32[4,8,128]{2,1,0:T(8,128)S(1)}, u32[]{:S(2)}, u32[]{:S(2)}) async-start(f32[4,8,128]{2,1,0:T(8,128)} %get-tuple-element.46), calls=%async_computation.2 | async-start | bytes 32768 | tf_op jit(solution)/shard_map/all_to_all | solution.py:181
  107.4 5.4 %collective-permute-start.9 = (f32[2,24,1,512]{3,2,1,0:T(1,128)S(1)}, f32[2,24,1,512]{3,2,1,0:T(1,128)S(1)}, u32[]{:S(2)}, u32[]{:S(2)}) collective-permute-start(f32[2,24,1,512]{3,2,1,0:T(1,128)S(1)} %get-tuple-element.36), channel_id=1, source_target_pairs={{1,0},{2,1},{3,2},{8,3},{9,8},{10,9},{11,10},{16,11},{17,16},{18,1... | collective-permute-start | bytes 294920 | tf_op jit(solution)/shard_map/ppermute | solution.py:27
  110.8 8.3 %collective-permute-start.8 = (f32[2,24,1,512]{3,2,1,0:T(1,128)S(1)}, f32[2,24,1,512]{3,2,1,0:T(1,128)S(1)}, u32[]{:S(2)}, u32[]{:S(2)}) collective-permute-start(f32[2,24,1,512]{3,2,1,0:T(1,128)S(1)} %get-tuple-element.35), channel_id=1, source_target_pairs={{0,1},{1,2},{2,3},{3,8},{8,9},{9,10},{10,11},{11,16},{16,17},{17,1... | collective-permute-start | bytes 294920 | tf_op jit(solution)/shard_map/ppermute | solution.py:26
  119.4 10.7 %collective-permute-start.11 = (f32[2,24,10,1]{3,2,1,0:T(8,128)S(1)}, f32[2,24,10,1]{3,2,1,0:T(8,128)S(1)}, u32[]{:S(2)}, u32[]{:S(2)}) collective-permute-start(f32[2,24,10,1]{3,2,1,0:T(8,128)S(1)} %get-tuple-element.32), channel_id=1, source_target_pairs={{4,0},{5,1},{6,2},{7,3},{12,8},{13,9},{14,10},{15,11},{20,16},{21,... | collective-permute-start | bytes 5768 | tf_op jit(solution)/shard_map/ppermute | solution.py:27
  120.7 11.1 %collective-permute-start.10 = (f32[2,24,10,1]{3,2,1,0:T(8,128)S(1)}, f32[2,24,10,1]{3,2,1,0:T(8,128)S(1)}, u32[]{:S(2)}, u32[]{:S(2)}) collective-permute-start(f32[2,24,10,1]{3,2,1,0:T(8,128)S(1)} %get-tuple-element.31), channel_id=1, source_target_pairs={{0,4},{1,5},{2,6},{3,7},{8,12},{9,13},{10,14},{11,15},{16,20},{17,... | collective-permute-start | bytes 5768 | tf_op jit(solution)/shard_map/ppermute | solution.py:26
where the time goes:
time: 138 us; the launch traced here: 136 us
  starting transfers between devices  52.4 us (38%)
  other arithmetic  48.3 us (35%)
  waiting for transfers between devices  27.7 us (20%)
  local copies, waits for them, and re-layouts  6.96 us (5%)
    mul x1, other arithmetic, closures(): conductivity * jnp.sqrt(saturation)  26.2 us
    ppermute x6, starting transfers between devices, with_halo(): before = lax.ppermute(last, axis, up)  26.1 us
    ppermute x6, starting transfers between devices, with_halo(): after = lax.ppermute(leading, axis, down)  14.4 us
    another operation x1, other arithmetic, local(): jnp.stack([head, conduct])  11.8 us
    ppermute x6, waiting for transfers between devices, with_halo(): after = lax.ppermute(leading, axis, down)  10.4 us
    ppermute x6, waiting for transfers between devices, with_halo(): before = lax.ppermute(last, axis, up)  9.1 us
    all_to_all x1, starting transfers between devices, local(): lax.all_to_all(top_conduct, 'gy', split_axis=1, concat_axis=0, tiled=True)  5.41 us
    slice x4, local copies, waits for them, and re-layouts, lookup(): filled = jnp.where(soil_class == kind_number, table[kind_number], filled)  4.97 us
  transfers between devices with their start and end apart: 15, of which 8 were waited for; matrix products, arithmetic and copies ran while one was open for 4% of the time, Pallas kernels for 0%

commit v1 on v0

--- a/solution.py
+++ b/solution.py
@@ -14,6 +14,12 @@
 SURFACE_STEP = 0.3
 LEAKANCE = 0.5
 SOURCE_GAIN = 1.0
+
+
+def stacked_exchange(block, axis, split, join):
+    parts = jnp.split(block, lax.axis_size(axis), axis=split)
+    arrived = lax.all_to_all(jnp.stack(parts), axis, 0, 0)
+    return jnp.concatenate(arrived, axis=join)
 
 
 def with_halo(shard, sides, width):
@@ -156,7 +162,7 @@
     )
     top_conduct = conduct[0]
     top, top_surface = (
-        lax.all_to_all(pressure[0], "gy", split_axis=1, concat_axis=0, tiled=True),
+        stacked_exchange(pressure[0], "gy", 1, 0),
         lax.all_to_all(top_conduct, "gy", split_axis=1, concat_axis=0, tiled=True),
     )
     leak = LEAKANCE * land_mask.astype(jnp.float32) * top_surface

time: 138 us -> 138 us (level)
  no operation moved by 1% of the time
where the time goes in v1:
time: 138 us; the launch traced here: 137 us
  starting transfers between devices  52.4 us (38%)
  other arithmetic  49 us (36%)
  waiting for transfers between devices  27.7 us (20%)
  local copies, waits for them, and re-layouts  6.39 us (5%)
    mul x1, other arithmetic, closures(): conductivity * jnp.sqrt(saturation)  26.2 us
    ppermute x6, starting transfers between devices, with_halo(): before = lax.ppermute(last, axis, up)  26.1 us
    ppermute x6, starting transfers between devices, with_halo(): after = lax.ppermute(leading, axis, down)  14.4 us
    another operation x1, other arithmetic, local(): jnp.stack([head, conduct])  11.9 us
    ppermute x6, waiting for transfers between devices, with_halo(): after = lax.ppermute(leading, axis, down)  10.4 us
    ppermute x6, waiting for transfers between devices, with_halo(): before = lax.ppermute(last, axis, up)  9.1 us
    all_to_all x1, starting transfers between devices, local(): lax.all_to_all(top_conduct, 'gy', split_axis=1, concat_axis=0, tiled=True)  5.41 us
    slice x4, local copies, waits for them, and re-layouts, lookup(): filled = jnp.where(soil_class == kind_number, table[kind_number], filled)  4.98 us
  transfers between devices with their start and end apart: 15, of which 8 were waited for; matrix products, arithmetic and copies ran while one was open for 4% of the time, Pallas kernels for 0%

profile of v1, /device:TPU:1, one launch (start us, length us, event | category | flops | bytes accessed | tf_op | source)
XLA Modules:
  0.0 136.6 jit_solution(4487403456805375125)
XLA Ops:
  0.7 1.8 %fusion.114 = (f32[1]{0:T(128)}, f32[1]{0:T(128)}, f32[1]{0:T(128)}, f32[1]{0:T(128)}, f32[1]{0:T(128)}, /*index=5*/f32[1]{0:T(128)}, f32[1]{0:T(128)}, f32[1]{0...) fusion(f32[12]{0:T(128)} %param.15), kind=kLoop, calls=%fused_computation.236 | loop fusion | bytes 96 | tf_op jit(solution)/shard_map/slice | solution.py:43
  2.5 1.8 %fusion.113 = (f32[1]{0:T(128)}, f32[1]{0:T(128)}, f32[1]{0:T(128)}, f32[1]{0:T(128)}, f32[1]{0:T(128)}, /*index=5*/f32[1]{0:T(128)}, f32[1]{0:T(128)}, f32[1]{0...) fusion(f32[12]{0:T(128)} %param.17), kind=kLoop, calls=%fused_computation.235 | loop fusion | bytes 96 | tf_op jit(solution)/shard_map/slice | solution.py:43
  4.9 0.7 fusion.112
  5.6 26.2 %multiply_multiply_fusion = (f32[24,8,512]{2,1,0:T(8,128)S(1)}, f32[24,8,512]{2,1,0:T(8,128)S(1)}, f32[24,8,512]{2,1,0:T(8,128)S(1)}, f32[24,8,512]{2,1,0:T(8,12...) fusion(f32[24,8,512]{2,1,0:T(8,128)} %param.12, ...), kind=kLoop, calls=%fused_computation.100 | loop fusion | flops 6094848 | bytes 3539088 | tf_op jit(solution)/shard_map/mul | solution.py:59
  32.5 5.4 %all-to-all-start = ((f32[8,4,128]{2,0,1:T(8,128)}), f32[8,4,128]{2,0,1:T(8,128)S(1)}, u32[]{:S(2)}, u32[]{:S(2)}) async-start(f32[8,4,128]{2,0,1:T(8,128)} %slice_bitcast_fusion.10), calls=%async_computation | async-start | bytes 32768 | tf_op jit(solution)/shard_map/all_to_all | solution.py:166
  38.6 3.8 %all-to-all-done = f32[8,4,128]{2,0,1:T(8,128)S(1)} async-done(((f32[8,4,128]{2,0,1:T(8,128)}), f32[8,4,128]{2,0,1:T(8,128)S(1)}, u32[]{:S(2)}, u32[]{:S(2)}) %all-to-all-start) | async-done | bytes 16416 | tf_op jit(solution)/shard_map/all_to_all | solution.py:166
  42.3 3.2 %all-to-all-start.1 = ((f32[4,8,128]{2,1,0:T(8,128)}), f32[4,8,128]{2,1,0:T(8,128)S(1)}, u32[]{:S(2)}, u32[]{:S(2)}) async-start(f32[4,8,128]{2,1,0:T(8,128)} %pad_maximum_fusion.16), calls=%async_computation.1 | async-start | bytes 32768 | tf_op jit(solution)/shard_map/all_to_all | solution.py:21
  45.6 4.4 %all-to-all-done.1 = f32[4,8,128]{2,1,0:T(8,128)S(1)} async-done(((f32[4,8,128]{2,1,0:T(8,128)}), f32[4,8,128]{2,1,0:T(8,128)S(1)}, u32[]{:S(2)}, u32[]{:S(2)}) %all-to-all-start.1) | async-done | bytes 16416 | tf_op jit(solution)/shard_map/all_to_all | solution.py:21
  50.0 5.2 %collective-permute-start.5 = (f32[6,3,128]{2,1,0:T(4,128)S(1)}, f32[6,3,128]{2,1,0:T(4,128)S(1)}, u32[]{:S(2)}, u32[]{:S(2)}) collective-permute-start(f32[6,3,128]{2,1,0:T(4,128)S(1)} %get-tuple-element.50), channel_id=1, source_target_pairs={{8,0},{16,8},{24,16},{9,1},{17,9},{25,17},{10,2},{18,10},{26,18},{... | collective-permute-start | bytes 27656 | tf_op jit(solution)/shard_map/ppermute | solution.py:33
  55.2 3.0 %collective-permute-start.4 = (f32[6,3,128]{2,1,0:T(4,128)S(1)}, f32[6,3,128]{2,1,0:T(4,128)S(1)}, u32[]{:S(2)}, u32[]{:S(2)}) collective-permute-start(f32[6,3,128]{2,1,0:T(4,128)S(1)} %get-tuple-element.49), channel_id=1, source_target_pairs={{0,8},{8,16},{16,24},{1,9},{9,17},{17,25},{2,10},{10,18},{18,26},{... | collective-permute-start | bytes 27656 | tf_op jit(solution)/shard_map/ppermute | solution.py:32
  58.4 1.9 %collective-permute-start.1 = (f32[2,24,1,512]{3,2,1,0:T(1,128)S(1)}, f32[2,24,1,512]{3,2,1,0:T(1,128)S(1)}, u32[]{:S(2)}, u32[]{:S(2)}) collective-permute-start(f32[2,24,1,512]{3,2,1,0:T(1,128)S(1)} %get-tuple-element.38), channel_id=1, source_target_pairs={{1,0},{2,1},{3,2},{8,3},{9,8},{10,9},{11,10},{16,11},{17,16},{18,1... | collective-permute-start | bytes 294920 | tf_op jit(solution)/shard_map/ppermute | solution.py:33
  60.3 3.4 %collective-permute-start = (f32[2,24,1,512]{3,2,1,0:T(1,128)S(1)}, f32[2,24,1,512]{3,2,1,0:T(1,128)S(1)}, u32[]{:S(2)}, u32[]{:S(2)}) collective-permute-start(f32[2,24,1,512]{3,2,1,0:T(1,128)S(1)} %get-tuple-element.37), channel_id=1, source_target_pairs={{0,1},{1,2},{2,3},{3,8},{8,9},{9,10},{10,11},{11,16},{16,17},{17,1... | collective-permute-start | bytes 294920 | tf_op jit(solution)/shard_map/ppermute | solution.py:32
  63.8 1.3 collective-permute-start.7
  65.1 4.0 %collective-permute-start.6 = (f32[6,38,3]{2,1,0:T(8,128)S(1)}, f32[6,38,3]{2,1,0:T(8,128)S(1)}, u32[]{:S(2)}, u32[]{:S(2)}) collective-permute-start(f32[6,38,3]{2,1,0:T(8,128)S(1)} %get-tuple-element.47), channel_id=1, source_target_pairs={{0,1},{1,2},{2,3},{3,4},{4,5},{5,6},{6,7},{8,9},{9,10},{10,11},{11... | collective-permute-start | bytes 8216 | tf_op jit(solution)/shard_map/ppermute | solution.py:32
  69.8 2.2 %collective-permute-done.7 = f32[6,38,3]{2,1,0:T(8,128)S(1)} collective-permute-done((f32[6,38,3]{2,1,0:T(8,128)S(1)}, f32[6,38,3]{2,1,0:T(8,128)S(1)}, u32[]{:S(2)}, u32[]{:S(2)}) %collective-permute-start.7) | collective-permute-done | bytes 2768 | tf_op jit(solution)/shard_map/ppermute | solution.py:33
  74.0 1.3 collective-permute-start.3
  75.3 9.5 %collective-permute-start.2 = (f32[2,24,10,1]{3,2,1,0:T(8,128)S(1)}, f32[2,24,10,1]{3,2,1,0:T(8,128)S(1)}, u32[]{:S(2)}, u32[]{:S(2)}) collective-permute-start(f32[2,24,10,1]{3,2,1,0:T(8,128)S(1)} %get-tuple-element.33), channel_id=1, source_target_pairs={{0,4},{1,5},{2,6},{3,7},{8,12},{9,13},{10,14},{11,15},{16,20},{17,... | collective-permute-start | bytes 5768 | tf_op jit(solution)/shard_map/ppermute | solution.py:32
  84.8 0.7 fusion.96
  85.5 3.2 %all-to-all-start.2 = ((f32[4,8,128]{2,1,0:T(8,128)}), f32[4,8,128]{2,1,0:T(8,128)S(1)}, u32[]{:S(2)}, u32[]{:S(2)}) async-start(f32[4,8,128]{2,1,0:T(8,128)} %get-tuple-element.46), calls=%async_computation.2 | async-start | bytes 32768 | tf_op jit(solution)/shard_map/all_to_all | solution.py:187
  88.8 3.2 %collective-permute-done.3 = f32[2,24,10,1]{3,2,1,0:T(8,128)S(1)} collective-permute-done((f32[2,24,10,1]{3,2,1,0:T(8,128)S(1)}, f32[2,24,10,1]{3,2,1,0:T(8,128)S(1)}, u32[]{:S(2)}, u32[]{:S(2)}) %collective-permute-start.3) | collective-permute-done | bytes 1952 | tf_op jit(solution)/shard_map/ppermute | solution.py:33
  92.0 0.9 collective-permute-done.2
  92.9 2.4 %pad_maximum_fusion = f32[2,24,10,514]{3,2,1,0:T(8,128)S(1)} fusion(f32[2,24,10,1]{3,2,1,0:T(8,128)S(1)} %collective-permute-done.3, f32[2,24,1,512]{3,2,1,0:T(1,128)} %copy-done.1, f32[1,24,8,512]{3,2,1,0:T(8,128)S(1)} %bitcast.124, f32[1,24,8,512]{3,2,1,0:T(8,128)S(1)} %bitcast.118, f32[2,24,1,512]{3,2,1,0:T(1,128)} %copy-done.2, ...), kind=kLoop, calls=%fused_computation | loop fusion | flops 1233600 | bytes 1973760 | tf_op jit(solution)/shard_map/concatenate | solution.py:34
  95.4 11.9 %multiply_bitcast_fusion = (f32[1,24,8,512]{3,2,1,0:T(8,128)S(1)}, f32[24,8,512]{2,1,0:T(8,128)S(1)}, f32[24,8,512]{2,1,0:T(8,128)S(1)}) fusion(f32[24,8,512]{2,1,0:T(8,128)S(1)} %get-tuple-element.14, f32[24,8,512]{2,1,0:T(8,128)S(1)} %get-tuple-element.13, f32[24,8,512]{2,1,0:T(8,128)S(1)} %get-tuple-element.12, f32[1,8,512]{2,1,0:T(8,128)S(1)} %bitcast.125, ...), kind=kLoop, calls=%fused_computation.94 | loop fusion | flops 7667712 | bytes 9846832 | tf_op jit(solution)/shard_map/stack | solution.py:191
  107.4 3.4 %collective-permute-start.9 = (f32[2,24,1,512]{3,2,1,0:T(1,128)S(1)}, f32[2,24,1,512]{3,2,1,0:T(1,128)S(1)}, u32[]{:S(2)}, u32[]{:S(2)}) collective-permute-start(f32[2,24,1,512]{3,2,1,0:T(1,128)S(1)} %get-tuple-element.36), channel_id=1, source_target_pairs={{1,0},{2,1},{3,2},{8,3},{9,8},{10,9},{11,10},{16,11},{17,16},{18,1... | collective-permute-start | bytes 294920 | tf_op jit(solution)/shard_map/ppermute | solution.py:33
  110.9 1.9 %collective-permute-start.8 = (f32[2,24,1,512]{3,2,1,0:T(1,128)S(1)}, f32[2,24,1,512]{3,2,1,0:T(1,128)S(1)}, u32[]{:S(2)}, u32[]{:S(2)}) collective-permute-start(f32[2,24,1,512]{3,2,1,0:T(1,128)S(1)} %get-tuple-element.35), channel_id=1, source_target_pairs={{0,1},{1,2},{2,3},{3,8},{8,9},{9,10},{10,11},{11,16},{16,17},{17,1... | collective-permute-start | bytes 294920 | tf_op jit(solution)/shard_map/ppermute | solution.py:32
  112.8 6.4 %collective-permute-done.8 = f32[2,24,1,512]{3,2,1,0:T(1,128)S(1)} collective-permute-done((f32[2,24,1,512]{3,2,1,0:T(1,128)S(1)}, f32[2,24,1,512]{3,2,1,0:T(1,128)S(1)}, u32[]{:S(2)}, u32[]{:S(2)}) %collective-permute-start.8) | collective-permute-done | bytes 98336 | tf_op jit(solution)/shard_map/ppermute | solution.py:32
  119.5 1.3 collective-permute-start.11
  120.8 4.3 %collective-permute-start.10 = (f32[2,24,10,1]{3,2,1,0:T(8,128)S(1)}, f32[2,24,10,1]{3,2,1,0:T(8,128)S(1)}, u32[]{:S(2)}, u32[]{:S(2)}) collective-permute-start(f32[2,24,10,1]{3,2,1,0:T(8,128)S(1)} %get-tuple-element.31), channel_id=1, source_target_pairs={{0,4},{1,5},{2,6},{3,7},{8,12},{9,13},{10,14},{11,15},{16,20},{17,... | collective-permute-start | bytes 5768 | tf_op jit(solution)/shard_map/ppermute | solution.py:32
  125.1 5.0 %collective-permute-done.11 = f32[2,24,10,1]{3,2,1,0:T(8,128)S(1)} collective-permute-done((f32[2,24,10,1]{3,2,1,0:T(8,128)S(1)}, f32[2,24,10,1]{3,2,1,0:T(8,128)S(1)}, u32[]{:S(2)}, u32[]{:S(2)}) %collective-permute-start.11) | collective-permute-done | bytes 1952 | tf_op jit(solution)/shard_map/ppermute | solution.py:33
  130.1 1.8 %collective-permute-done.10 = f32[2,24,10,1]{3,2,1,0:T(8,128)S(1)} collective-permute-done((f32[2,24,10,1]{3,2,1,0:T(8,128)S(1)}, f32[2,24,10,1]{3,2,1,0:T(8,128)S(1)}, u32[]{:S(2)}, u32[]{:S(2)}) %collective-permute-start.10) | collective-permute-done | bytes 1952 | tf_op jit(solution)/shard_map/ppermute | solution.py:32
  131.9 1.4 %pad_maximum_fusion.1 = f32[2,24,10,514]{3,2,1,0:T(8,128)S(1)} fusion(f32[2,24,10,1]{3,2,1,0:T(8,128)S(1)} %collective-permute-done.11, f32[2,24,1,512]{3,2,1,0:T(1,128)S(1)} %collective-permute-done.9, f32[1,24,8,512]{3,2,1,0:T(8,128)S(1)} %get-tuple-element.5, f32[1,24,8,512]{3,2,1,0:T(8,128)S(1)} %bitcast.121, ...), kind=kLoop, calls=%fused_computation.1 | loop fusion | flops 1233600 | bytes 1973760 | tf_op jit(solution)/shard_map/concatenate | solution.py:34
  133.5 3.1 %fusion.1 = f32[24,8,512]{2,1,0:T(8,128)} fusion(f32[1,8,512]{2,1,0:T(8,128)S(1)} %bitcast.126, f32[24,10,514]{2,1,0:T(8,128)S(1)} %get-tuple-element.28, f32[24,10,514]{2,1,0:T(8,128)S(1)} %get-tuple-element.27, f32[24,8,512]{2,1,0:T(8,128)S(1)} %get-tuple-element.7, f32[24,8,512]{2,1,0:T(8,128)S(1)} %get-tuple-element.14, ...), kind=kLoop, calls=%fused_computation.17 | loop fusion | flops 5996544 | bytes 8273920 | tf_op jit(solution)/shard_map/div | solution.py:94
  (59 shorter events, 5.5 us)
Async XLA Ops:
  0.6 37.2 %copy-start = (f32[24,8,512]{2,1,0:T(8,128)S(1)}, f32[24,8,512]{2,1,0:T(8,128)}, u32[]{:S(2)}) copy-start(f32[24,8,512]{2,1,0:T(8,128)} %param.12) | copy-start | bytes 1179652
  0.6 37.2 %copy-start.7 = (f32[32,128]{1,0:T(8,128)S(1)}, f32[32,128]{1,0:T(8,128)}, u32[]{:S(2)}) copy-start(f32[32,128]{1,0:T(8,128)} %param.18) | copy-start | bytes 49156
  0.7 37.3 %copy-start.8 = (f32[32,128]{1,0:T(8,128)S(1)}, f32[32,128]{1,0:T(8,128)}, u32[]{:S(2)}) copy-start(f32[32,128]{1,0:T(8,128)} %param.19) | copy-start | bytes 49156
  0.7 37.3 %copy-start.4 = (f32[32,128]{1,0:T(8,128)S(1)}, f32[32,128]{1,0:T(8,128)}, u32[]{:S(2)}) copy-start(f32[32,128]{1,0:T(8,128)} %param.20) | copy-start | bytes 49156
  0.7 37.3 %copy-start.5 = (s32[32,128]{1,0:T(8,128)S(1)}, s32[32,128]{1,0:T(8,128)}, u32[]{:S(2)}) copy-start(s32[32,128]{1,0:T(8,128)} %param.23) | copy-start | bytes 49156
  5.6 39.9 %copy-start.6 = (s32[32,128]{1,0:T(8,128)S(1)}, s32[32,128]{1,0:T(8,128)}, u32[]{:S(2)}) copy-start(s32[32,128]{1,0:T(8,128)} %param.22) | copy-start | bytes 49156
  5.6 44.4 %copy-start.9 = (f32[32,128]{1,0:T(8,128)S(1)}, f32[32,128]{1,0:T(8,128)}, u32[]{:S(2)}) copy-start(f32[32,128]{1,0:T(8,128)} %param.21) | copy-start | bytes 49156
  31.8 37.3 %copy-start.3 = (f32[12]{0:T(128)S(1)}, f32[12]{0:T(128)}, u32[]{:S(2)}) copy-start(f32[12]{0:T(128)} %param.14) | copy-start | bytes 148
  32.5 9.9 %all-to-all-start = ((f32[8,4,128]{2,0,1:T(8,128)}), f32[8,4,128]{2,0,1:T(8,128)S(1)}, u32[]{:S(2)}, u32[]{:S(2)}) async-start(f32[8,4,128]{2,0,1:T(8,128)} %slice_bitcast_fusion.10), calls=%async_computation | async-start | bytes 32768 | tf_op jit(solution)/shard_map/all_to_all | solution.py:166
  42.3 7.7 %all-to-all-start.1 = ((f32[4,8,128]{2,1,0:T(8,128)}), f32[4,8,128]{2,1,0:T(8,128)S(1)}, u32[]{:S(2)}, u32[]{:S(2)}) async-start(f32[4,8,128]{2,1,0:T(8,128)} %pad_maximum_fusion.16), calls=%async_computation.1 | async-start | bytes 32768 | tf_op jit(solution)/shard_map/all_to_all | solution.py:21
  50.0 13.6 %collective-permute-start.5 = (f32[6,3,128]{2,1,0:T(4,128)S(1)}, f32[6,3,128]{2,1,0:T(4,128)S(1)}, u32[]{:S(2)}, u32[]{:S(2)}) collective-permute-start(f32[6,3,128]{2,1,0:T(4,128)S(1)} %get-tuple-element.50), channel_id=1, source_target_pairs={{8,0},{16,8},{24,16},{9,1},{17,9},{25,17},{10,2},{18,10},{26,18},{... | collective-permute-start | bytes 27656 | tf_op jit(solution)/shard_map/ppermute | solution.py:33
  55.2 8.5 %collective-permute-start.4 = (f32[6,3,128]{2,1,0:T(4,128)S(1)}, f32[6,3,128]{2,1,0:T(4,128)S(1)}, u32[]{:S(2)}, u32[]{:S(2)}) collective-permute-start(f32[6,3,128]{2,1,0:T(4,128)S(1)} %get-tuple-element.49), channel_id=1, source_target_pairs={{0,8},{8,16},{16,24},{1,9},{9,17},{17,25},{2,10},{10,18},{18,26},{... | collective-permute-start | bytes 27656 | tf_op jit(solution)/shard_map/ppermute | solution.py:32
  58.4 15.0 %collective-permute-start.1 = (f32[2,24,1,512]{3,2,1,0:T(1,128)S(1)}, f32[2,24,1,512]{3,2,1,0:T(1,128)S(1)}, u32[]{:S(2)}, u32[]{:S(2)}) collective-permute-start(f32[2,24,1,512]{3,2,1,0:T(1,128)S(1)} %get-tuple-element.38), channel_id=1, source_target_pairs={{1,0},{2,1},{3,2},{8,3},{9,8},{10,9},{11,10},{16,11},{17,16},{18,1... | collective-permute-start | bytes 294920 | tf_op jit(solution)/shard_map/ppermute | solution.py:33
  60.3 13.1 %collective-permute-start = (f32[2,24,1,512]{3,2,1,0:T(1,128)S(1)}, f32[2,24,1,512]{3,2,1,0:T(1,128)S(1)}, u32[]{:S(2)}, u32[]{:S(2)}) collective-permute-start(f32[2,24,1,512]{3,2,1,0:T(1,128)S(1)} %get-tuple-element.37), channel_id=1, source_target_pairs={{0,1},{1,2},{2,3},{3,8},{8,9},{9,10},{10,11},{11,16},{16,17},{17,1... | collective-permute-start | bytes 294920 | tf_op jit(solution)/shard_map/ppermute | solution.py:32
  63.8 8.2 %collective-permute-start.7 = (f32[6,38,3]{2,1,0:T(8,128)S(1)}, f32[6,38,3]{2,1,0:T(8,128)S(1)}, u32[]{:S(2)}, u32[]{:S(2)}) collective-permute-start(f32[6,38,3]{2,1,0:T(8,128)S(1)} %get-tuple-element.48), channel_id=1, source_target_pairs={{1,0},{2,1},{3,2},{4,3},{5,4},{6,5},{7,6},{9,8},{10,9},{11,10},{12... | collective-permute-start | bytes 8216 | tf_op jit(solution)/shard_map/ppermute | solution.py:33
  65.1 6.9 %collective-permute-start.6 = (f32[6,38,3]{2,1,0:T(8,128)S(1)}, f32[6,38,3]{2,1,0:T(8,128)S(1)}, u32[]{:S(2)}, u32[]{:S(2)}) collective-permute-start(f32[6,38,3]{2,1,0:T(8,128)S(1)} %get-tuple-element.47), channel_id=1, source_target_pairs={{0,1},{1,2},{2,3},{3,4},{4,5},{5,6},{6,7},{8,9},{9,10},{10,11},{11... | collective-permute-start | bytes 8216 | tf_op jit(solution)/shard_map/ppermute | solution.py:32
  73.4 0.6 copy-start.1
  73.4 0.7 copy-start.2
  74.0 17.9 %collective-permute-start.3 = (f32[2,24,10,1]{3,2,1,0:T(8,128)S(1)}, f32[2,24,10,1]{3,2,1,0:T(8,128)S(1)}, u32[]{:S(2)}, u32[]{:S(2)}) collective-permute-start(f32[2,24,10,1]{3,2,1,0:T(8,128)S(1)} %get-tuple-element.34), channel_id=1, source_target_pairs={{4,0},{5,1},{6,2},{7,3},{12,8},{13,9},{14,10},{15,11},{20,16},{21,... | collective-permute-start | bytes 5768 | tf_op jit(solution)/shard_map/ppermute | solution.py:33
  75.3 17.6 %collective-permute-start.2 = (f32[2,24,10,1]{3,2,1,0:T(8,128)S(1)}, f32[2,24,10,1]{3,2,1,0:T(8,128)S(1)}, u32[]{:S(2)}, u32[]{:S(2)}) collective-permute-start(f32[2,24,10,1]{3,2,1,0:T(8,128)S(1)} %get-tuple-element.33), channel_id=1, source_target_pairs={{0,4},{1,5},{2,6},{3,7},{8,12},{9,13},{10,14},{11,15},{16,20},{17,... | collective-permute-start | bytes 5768 | tf_op jit(solution)/shard_map/ppermute | solution.py:32
  85.5 9.9 %all-to-all-start.2 = ((f32[4,8,128]{2,1,0:T(8,128)}), f32[4,8,128]{2,1,0:T(8,128)S(1)}, u32[]{:S(2)}, u32[]{:S(2)}) async-start(f32[4,8,128]{2,1,0:T(8,128)} %get-tuple-element.46), calls=%async_computation.2 | async-start | bytes 32768 | tf_op jit(solution)/shard_map/all_to_all | solution.py:187
  107.4 5.4 %collective-permute-start.9 = (f32[2,24,1,512]{3,2,1,0:T(1,128)S(1)}, f32[2,24,1,512]{3,2,1,0:T(1,128)S(1)}, u32[]{:S(2)}, u32[]{:S(2)}) collective-permute-start(f32[2,24,1,512]{3,2,1,0:T(1,128)S(1)} %get-tuple-element.36), channel_id=1, source_target_pairs={{1,0},{2,1},{3,2},{8,3},{9,8},{10,9},{11,10},{16,11},{17,16},{18,1... | collective-permute-start | bytes 294920 | tf_op jit(solution)/shard_map/ppermute | solution.py:33
  110.9 8.3 %collective-permute-start.8 = (f32[2,24,1,512]{3,2,1,0:T(1,128)S(1)}, f32[2,24,1,512]{3,2,1,0:T(1,128)S(1)}, u32[]{:S(2)}, u32[]{:S(2)}) collective-permute-start(f32[2,24,1,512]{3,2,1,0:T(1,128)S(1)} %get-tuple-element.35), channel_id=1, source_target_pairs={{0,1},{1,2},{2,3},{3,8},{8,9},{9,10},{10,11},{11,16},{16,17},{17,1... | collective-permute-start | bytes 294920 | tf_op jit(solution)/shard_map/ppermute | solution.py:32
  119.5 10.7 %collective-permute-start.11 = (f32[2,24,10,1]{3,2,1,0:T(8,128)S(1)}, f32[2,24,10,1]{3,2,1,0:T(8,128)S(1)}, u32[]{:S(2)}, u32[]{:S(2)}) collective-permute-start(f32[2,24,10,1]{3,2,1,0:T(8,128)S(1)} %get-tuple-element.32), channel_id=1, source_target_pairs={{4,0},{5,1},{6,2},{7,3},{12,8},{13,9},{14,10},{15,11},{20,16},{21,... | collective-permute-start | bytes 5768 | tf_op jit(solution)/shard_map/ppermute | solution.py:33
  120.8 11.1 %collective-permute-start.10 = (f32[2,24,10,1]{3,2,1,0:T(8,128)S(1)}, f32[2,24,10,1]{3,2,1,0:T(8,128)S(1)}, u32[]{:S(2)}, u32[]{:S(2)}) collective-permute-start(f32[2,24,10,1]{3,2,1,0:T(8,128)S(1)} %get-tuple-element.31), channel_id=1, source_target_pairs={{0,4},{1,5},{2,6},{3,7},{8,12},{9,13},{10,14},{11,15},{16,20},{17,... | collective-permute-start | bytes 5768 | tf_op jit(solution)/shard_map/ppermute | solution.py:32
